TPU v7x, 16 devices: a whole 2x2x2 slice. The times are simulated.
16 devices in a mesh: fsdp: 2 (over z), ep: 8 (over y, x, core).
Axes of the slice: x: 2, y: 2, z: 2, core: 2. Of those that a mesh axis runs over, the one named last changes fastest.
Arguments:
- x_tok: bfloat16 [32768, 512], P(('fsdp', 'ep'))
- dy_tok: bfloat16 [32768, 512], P(('fsdp', 'ep'))
- expert_ids: int32 [32768, 6], P(('fsdp', 'ep'))
- route_w: float32 [32768, 6], P(('fsdp', 'ep'))
- w_gate: bfloat16 [160, 512, 384], P('ep', 'fsdp')
- w_up: bfloat16 [160, 512, 384], P('ep', 'fsdp')
- w_down: bfloat16 [160, 384, 512], P('ep', None, 'fsdp')
Outputs:
- output 1: bfloat16 [32768, 512], P(('fsdp', 'ep'))
- output 2: float32 [32768, 6], P(('fsdp', 'ep'))
- output 3: float32 [160, 512, 384], P('ep', 'fsdp')
- output 4: float32 [160, 512, 384], P('ep', 'fsdp')
- output 5: float32 [160, 384, 512], P('ep', None, 'fsdp')
All inputs are finite; a program needn't handle non-finite values.
Results may differ from a plain program's by a relative error of at most 0.00867669.
Values are sent between devices in bfloat16 or wider.
A program may use at most 1 GiB of HBM per device.

v0:
```python
import jax
import jax.numpy as jnp
from jax import lax
from jax.sharding import PartitionSpec as P

CAP_FACTOR = 3


def capacity_of(tok_dev, top_k, experts):
    return max(8, ((CAP_FACTOR * tok_dev * top_k // experts + 7) // 8) * 8)


def route_slots(ids_dev, experts, capacity):
    n_pairs = ids_dev.shape[0]
    n_slots = experts * capacity
    onehot = (ids_dev[:, None] == jnp.arange(experts, dtype=jnp.int32)[None, :]).astype(jnp.int32)
    before = jnp.cumsum(onehot, axis=0) - onehot
    position = jnp.sum(before * onehot, axis=1)
    dest_slot = jnp.where(position < capacity, ids_dev * capacity + position, n_slots)
    held = jax.ops.segment_sum(jnp.arange(1, n_pairs + 1, dtype=jnp.int32), dest_slot, num_segments=n_slots + 1)[:n_slots]
    slot_src = jnp.where(held > 0, held - 1, n_pairs)
    return dest_slot, slot_src


def swiglu_grads(pre_gate, pre_up, grad_hidden):
    sigma = jax.nn.sigmoid(pre_gate)
    grad_gate = grad_hidden * pre_up * sigma * (1.0 + pre_gate * (1.0 - sigma))
    grad_up = grad_hidden * pre_gate * sigma
    return grad_gate.astype(jnp.bfloat16), grad_up.astype(jnp.bfloat16)


def expert_backward(x_rows, dy_rows, gate_rows, w_gate_full, w_up_full, w_down_full):
    pre_gate = jnp.einsum("secd,edf->secf", x_rows, w_gate_full, preferred_element_type=jnp.float32)
    pre_up = jnp.einsum("secd,edf->secf", x_rows, w_up_full, preferred_element_type=jnp.float32)
    hidden = (jax.nn.silu(pre_gate) * pre_up).astype(jnp.bfloat16)
    y_rows = jnp.einsum("secf,efd->secd", hidden, w_down_full, preferred_element_type=jnp.float32)
    dy_wide = dy_rows.astype(jnp.float32)
    scaled_dy = (gate_rows[..., None] * dy_wide).astype(jnp.bfloat16)
    dr_rows = jnp.sum(dy_wide * y_rows, axis=-1)
    grad_hidden = jnp.einsum("secd,efd->secf", scaled_dy, w_down_full, preferred_element_type=jnp.float32)
    grad_gate, grad_up = swiglu_grads(pre_gate, pre_up, grad_hidden)
    dx_rows = (jnp.einsum("secf,edf->secd", grad_gate, w_gate_full, preferred_element_type=jnp.float32)
               + jnp.einsum("secf,edf->secd", grad_up, w_up_full, preferred_element_type=jnp.float32)).astype(jnp.bfloat16)
    dw_gate = jnp.einsum("secd,secf->edf", x_rows, grad_gate, preferred_element_type=jnp.float32)
    dw_up = jnp.einsum("secd,secf->edf", x_rows, grad_up, preferred_element_type=jnp.float32)
    dw_down = jnp.einsum("secf,secd->efd", hidden, scaled_dy, preferred_element_type=jnp.float32)
    return dx_rows, dr_rows, dw_gate, dw_up, dw_down


def take_rows(rows, row_ids):
    return jnp.take(rows, row_ids, axis=0, mode="fill", fill_value=0)


def solution(mesh):
    n_ep = mesh.shape["ep"]
    tok_spec = P(("fsdp", "ep"), None)
    spec_in = P("ep", "fsdp", None)
    spec_out = P("ep", None, "fsdp")

    def per_device(x_tok, dy_tok, expert_ids, route_w, w_gate, w_up, w_down):
        tok_dev, top_k = expert_ids.shape
        exp_local = w_gate.shape[0]
        d_model = x_tok.shape[1]
        experts = exp_local * n_ep
        capacity = capacity_of(tok_dev, top_k, experts)
        dest_slot, slot_src = route_slots(expert_ids.reshape(-1), experts, capacity)
        tok_of_slot = slot_src // top_k
        x_send = take_rows(x_tok, tok_of_slot)
        dy_send = take_rows(dy_tok, tok_of_slot)
        gate_send = take_rows(route_w.reshape(-1), slot_src)
        x_recv = lax.all_to_all(x_send, "ep", 0, 0, tiled=True).reshape(n_ep, exp_local, capacity, d_model)
        dy_recv = lax.all_to_all(dy_send, "ep", 0, 0, tiled=True).reshape(n_ep, exp_local, capacity, d_model)
        gate_recv = lax.all_to_all(gate_send, "ep", 0, 0, tiled=True).reshape(n_ep, exp_local, capacity)
        w_gate_full = lax.all_gather(w_gate, "fsdp", axis=1, tiled=True)
        w_up_full = lax.all_gather(w_up, "fsdp", axis=1, tiled=True)
        w_down_full = lax.all_gather(w_down, "fsdp", axis=2, tiled=True)
        dx_rows, dr_rows, dw_gate, dw_up, dw_down = expert_backward(
            x_recv, dy_recv, gate_recv, w_gate_full, w_up_full, w_down_full)
        dx_back = lax.all_to_all(dx_rows.reshape(n_ep * exp_local * capacity, d_model), "ep", 0, 0, tiled=True)
        dr_back = lax.all_to_all(dr_rows.reshape(-1), "ep", 0, 0, tiled=True)
        dx_pairs = take_rows(dx_back, dest_slot).reshape(tok_dev, top_k, d_model)
        grad_x = jnp.sum(dx_pairs.astype(jnp.float32), axis=1).astype(jnp.bfloat16)
        route_grad = take_rows(dr_back, dest_slot).reshape(tok_dev, top_k)
        grad_w_gate = lax.psum_scatter(dw_gate, "fsdp", scatter_dimension=1, tiled=True)
        grad_w_up = lax.psum_scatter(dw_up, "fsdp", scatter_dimension=1, tiled=True)
        grad_w_down = lax.psum_scatter(dw_down, "fsdp", scatter_dimension=2, tiled=True)
        return grad_x, route_grad, grad_w_gate, grad_w_up, grad_w_down

    return jax.shard_map(
        per_device, mesh=mesh,
        in_specs=(tok_spec, tok_spec, tok_spec, tok_spec, spec_in, spec_in, spec_out),
        out_specs=(tok_spec, tok_spec, spec_in, spec_in, spec_out),
        check_vma=False)
```

profile of v0, /device:TPU:0, one launch (start us, length us, event | category | flops | bytes accessed | tf_op | source)
XLA Modules:
  0.0 2533.0 jit_solution(13799567643678475880)
XLA Ops:
  7.2 1.3 copy.28
  8.5 0.7 eq.29
  9.2 0.7 eq.25
  9.9 1.0 broadcast_multiply_fusion
  11.0 0.1 copy.30
  11.1 6.2 fusion.25
  17.3 0.9 slice_bitcast_fusion
  18.2 0.2 reduce-window.9
  18.4 11.6 broadcast_add_fusion
  29.9 11.8 copy.31
  41.7 2.0 mul.64
  43.7 11.2 fusion.38
  54.9 0.7 compare_select_fusion.4
  55.6 64.5 %scatter_custom_fusion = s32[37121]{0:T(1024)S(1)} fusion(s32[12288]{0:T(1024)S(1)} %bitcast.122, s32[12288]{0:T(1024)S(1)} %iota_add_fusion, s32[]{:T(128)} %constant.48.clone.1), kind=kCustom, calls=%fused_computation.81 | custom fusion | flops 12288 | bytes 148488 | tf_op jit(solution)/shard_map/scatter-add | solution.py:20
  120.2 0.7 pad_clamp_fusion.1
  120.9 1.2 copy.33
  122.1 0.7 reshape.171
  122.8 190.7 %gather_fusion = f32[37120]{0:T(1024)S(1)} fusion(f32[12288]{0:T(1024)S(1)} %reshape.171, s32[37888]{0:T(1024)} %pad_clamp_fusion.1), kind=kCustom, calls=%fused_computation.2 | custom fusion | bytes 445440 | tf_op jit(solution)/shard_map/jit(_take)/gather | solution.py:51
  313.4 0.1 gather.22
  313.6 0.1 select_n.102
  313.7 0.8 copy.34
  314.6 5.5 all-to-all-start
  320.0 0.8 compare_and_fusion.1
  320.8 102.3 %gather_fusion.3 = bf16[37120,512]{1,0:T(8,128)(2,1)} fusion(bf16[2048,512]{1,0:T(8,128)(2,1)S(1)} %copy-done, s32[37888]{0:T(1024)S(1)} %pad_clamp_fusion), kind=kCustom, calls=%fused_computation.clone | custom fusion | bytes 76170240 | tf_op jit(solution)/shard_map/jit(_take)/gather | solution.py:51
  423.2 106.0 %gather_fusion.4 = bf16[37120,512]{1,0:T(8,128)(2,1)} fusion(bf16[2048,512]{1,0:T(8,128)(2,1)} %param.9, s32[37888]{0:T(1024)S(1)} %pad_clamp_fusion), kind=kCustom, calls=%fused_computation.1.clone | custom fusion | bytes 76170240 | tf_op jit(solution)/shard_map/jit(_take)/gather | solution.py:51
  529.2 49.9 %broadcast_select_fusion.1 = (bf16[37120,512]{1,0:T(8,128)(2,1)}, bf16[37120,512]{1,0:T(8,128)(2,1)}) fusion(bf16[37120,512]{1,0:T(8,128)(2,1)} %gather_fusion.3, pred[37120]{0:T(1024)(128)(4,1)S(1)} %copy-done.9, bf16[37120,512]{1,0:T(8,128)(2,1)} %gather_fusion.4), kind=kLoop, calls=%fused_computation.28 | loop fusion | flops 38010880 | bytes 152080640 | tf_op jit(solution)/shard_map/jit(_take)/select_n | solution.py:51
  579.0 423.2 %all_to_all.49 = bf16[8,4640,512]{2,1,0:T(8,128)(2,1)} all-to-all(bf16[8,4640,512]{2,1,0:T(8,128)(2,1)} %bitcast.115), channel_id=1, replica_groups=mesh['fsdp'=2,'ep'=8] {'ep'}, dimensions={0} | all-to-all | bytes 76021760 | tf_op jit(solution)/shard_map/all_to_all | solution.py:72
  1002.2 7.5 all-to-all-start.2
  1009.7 0.0 all-gather.4.cloned.1.call-start
  1009.7 0.7 all-gather.4.cloned.1.call-update
  1010.5 0.7 all-gather.6.cloned.1.call-update
  1011.2 0.7 all-gather.8.cloned.1.call-update
  1012.0 1.3 reduce.1
  1013.2 0.1 mul.65
  1013.4 97.5 %all-gather.4.cloned.1.call-done = bf16[20,384,512]{2,1,0:T(8,128)(2,1)} async-done(((bf16[20,384,256]{2,1,0:T(8,128)(2,1)}), bf16[20,384,512]{2,1,0:T(8,128)(2,1)}) %all-gather.4.cloned.1.call-update) | async-done | bytes 7864336 | tf_op jit(solution)/shard_map/all_gather | solution.py:76
  1110.9 40.4 %fusion.19 = f32[20,8,232,384]{3,2,1,0:T(8,128)} fusion(bf16[20,384,512]{2,1,0:T(8,128)(2,1)} %all-gather.4.cloned.1.call-done, f32[8,20,232]{2,1,0:T(8,128)S(1)} %mul.65, bf16[8,20,232,512]{3,2,1,0:T(8,128)(2,1)} %bitcast.116), kind=kOutput, calls=%fused_computation.35 | convolution fusion | flops 14653194240 | bytes 103040000 | tf_op jit(solution)/shard_map/secd,efd->secf/dot_general | solution.py:40
  1151.3 58.3 %all-gather.6.cloned.1.call-done = bf16[20,512,384]{2,1,0:T(8,128)(2,1)} async-done(((bf16[20,256,384]{2,1,0:T(8,128)(2,1)}), bf16[20,512,384]{2,1,0:T(8,128)(2,1)}) %all-gather.6.cloned.1.call-update) | async-done | bytes 7864336 | tf_op jit(solution)/shard_map/all_gather | solution.py:75
  1209.6 211.7 %all-to-all-done.2 = bf16[8,4640,512]{2,1,0:T(8,128)(2,1)} async-done(((bf16[8,4640,512]{2,1,0:T(8,128)(2,1)}), bf16[8,4640,512]{2,1,0:T(8,128)(2,1)}, u32[]{:S(2)}, u32[]{:S(2)}) %all-to-all-start.2) | async-done | bytes 38010912 | tf_op jit(solution)/shard_map/all_to_all | solution.py:71
  1421.4 38.7 %fusion.15 = f32[20,8,232,384]{3,2,1,0:T(8,128)} fusion(bf16[8,20,232,512]{3,2,1,0:T(8,128)(2,1)} %bitcast.10, bf16[20,512,384]{2,1,0:T(8,128)(2,1)} %all-gather.6.cloned.1.call-done), kind=kOutput, calls=%fused_computation.31 | convolution fusion | flops 14596177920 | bytes 102891520 | tf_op jit(solution)/shard_map/secd,edf->secf/dot_general | solution.py:34
  1460.1 82.6 %fusion.10 = (bf16[8,20,232,384]{3,2,0,1:T(8,128)(2,1)}, bf16[8,20,232,384]{3,2,0,1:T(8,128)(2,1)}, bf16[8,20,232,384]{3,2,0,1:T(8,128)(2,1)}) fusion(f32[20,8,232,384]{3,2,1,0:T(8,128)} %fusion.15, f32[20,8,232,384]{3,2,1,0:T(8,128)} %fusion.19, bf16[20,512,384]{2,1,0:T(8,128)(2,1)} %all-gather.8.cloned.1.call-done, bf16[8,20,232,512]{3,2,1,0:T(8,128)(2,1)} %bitcast.10), kind=kOutput, calls=%fused_computation.23 | convolution fusion | flops 14824243200 | bytes 245432320 | tf_op jit(solution)/shard_map/secd,edf->secf/dot_general | solution.py:33
  1542.7 32.9 %fusion.33 = f32[20,384,512]{2,1,0:T(8,128)} fusion(bf16[8,20,232,384]{3,2,0,1:T(8,128)(2,1)} %get-tuple-element.22, f32[8,20,232]{2,1,0:T(8,128)S(1)} %copy-done.8, bf16[8,20,232,512]{3,2,1,0:T(8,128)(2,1)} %bitcast.117), kind=kOutput, calls=%fused_computation.47 | convolution fusion | flops 14653194240 | bytes 82396160 | tf_op jit(solution)/shard_map/secf,secd->efd/dot_general | solution.py:46
  1575.6 0.0 reduce-scatter.6.cloned.1.call-start
  1575.7 33.8 %fusion.30 = f32[20,512,384]{2,1,0:T(8,128)} fusion(bf16[8,20,232,512]{3,2,1,0:T(8,128)(2,1)} %bitcast.10, bf16[8,20,232,384]{3,2,0,1:T(8,128)(2,1)} %get-tuple-element.24), kind=kOutput, calls=%fused_computation.46 | convolution fusion | flops 14596177920 | bytes 82247680 | tf_op jit(solution)/shard_map/secd,secf->edf/dot_general | solution.py:45
  1609.5 28.8 %fusion = f32[8,20,232]{2,0,1:T(8,128)S(1)} fusion(bf16[8,20,232,384]{3,2,0,1:T(8,128)(2,1)} %get-tuple-element.22, bf16[20,384,512]{2,1,0:T(8,128)(2,1)} %all-gather.4.cloned.1.call-done, bf16[8,20,232,512]{3,2,1,0:T(8,128)(2,1)} %bitcast.118), kind=kOutput, calls=%fused_computation.7 | convolution fusion | flops 14653157376 | bytes 74531840 | tf_op jit(solution)/shard_map/secf,efd->secd/dot_general | solution.py:36
  1638.3 0.1 copy.40
  1638.4 0.9 all_to_all.43
  1639.3 3.6 all-to-all-start.4
  1642.9 39.9 %fusion.39 = f32[20,8,232,512]{3,2,1,0:T(8,128)} fusion(bf16[8,20,232,384]{3,2,0,1:T(8,128)(2,1)} %get-tuple-element.23, bf16[20,512,384]{2,1,0:T(8,128)(2,1)} %all-gather.8.cloned.1.call-done), kind=kOutput, calls=%fused_computation.52 | convolution fusion | flops 14596177920 | bytes 112394240 | tf_op jit(solution)/shard_map/secf,edf->secd/dot_general | solution.py:42
  1682.9 48.6 %fusion.12 = bf16[8,20,232,512]{3,2,0,1:T(8,128)(2,1)} fusion(f32[20,8,232,512]{3,2,1,0:T(8,128)} %fusion.39, bf16[8,20,232,384]{3,2,0,1:T(8,128)(2,1)} %get-tuple-element.24, bf16[20,512,384]{2,1,0:T(8,128)(2,1)} %all-gather.6.cloned.1.call-done), kind=kOutput, calls=%fused_computation.26 | convolution fusion | flops 14634188800 | bytes 150405120 | tf_op jit(solution)/shard_map/secf,edf->secd/dot_general | solution.py:43
  1731.5 25.8 %copy.38 = bf16[8,20,232,512]{3,2,1,0:T(8,128)(2,1)} copy(bf16[8,20,232,512]{3,2,0,1:T(8,128)(2,1)} %fusion.12) | data formatting | bytes 76021760 | tf_op jit(solution)/shard_map/convert_element_type | solution.py:43
  1757.4 7.5 all-to-all-start.3
  1764.9 0.0 reduce-scatter.4.cloned.1.call-start
  1764.9 34.0 %fusion.27 = f32[20,512,384]{2,1,0:T(8,128)} fusion(bf16[8,20,232,512]{3,2,1,0:T(8,128)(2,1)} %bitcast.10, bf16[8,20,232,384]{3,2,0,1:T(8,128)(2,1)} %get-tuple-element.23), kind=kOutput, calls=%fused_computation.45 | convolution fusion | flops 14596177920 | bytes 82247680 | tf_op jit(solution)/shard_map/secd,secf->edf/dot_general | solution.py:44
  1799.0 1.0 reduce_sum.35
  1800.1 0.4 reduce.2
  1800.4 0.1 all_to_all.42
  1800.6 68.0 %gather_fusion.2 = f32[12288]{0:T(1024)S(1)} fusion(f32[37120]{0:T(1024)S(1)} %all_to_all.42, s32[12288]{0:T(1024)S(1)} %broadcast_clamp_fusion), kind=kCustom, calls=%fused_computation.4 | custom fusion | bytes 147456 | tf_op jit(solution)/shard_map/jit(_take)/gather | solution.py:51
  1868.6 2.0 gather.26
  1870.6 2.7 broadcast_select_fusion.2
  1873.3 2.2 copy.45
  1875.5 301.1 %all-to-all-done.3 = bf16[8,4640,512]{2,1,0:T(8,128)(2,1)} async-done(((bf16[8,4640,512]{2,1,0:T(8,128)(2,1)}), bf16[8,4640,512]{2,1,0:T(8,128)(2,1)}, u32[]{:S(2)}, u32[]{:S(2)}) %all-to-all-start.3) | async-done | bytes 38010912 | tf_op jit(solution)/shard_map/all_to_all | solution.py:79
  2176.6 308.2 %gather_fusion.1 = bf16[12288,512]{1,0:T(8,128)(2,1)} fusion(bf16[37120,512]{1,0:T(8,128)(2,1)} %bitcast.20, s32[12288]{0:T(1024)S(1)} %broadcast_clamp_fusion), kind=kCustom, calls=%fused_computation.3 | custom fusion | bytes 25214976 | tf_op jit(solution)/shard_map/jit(_take)/gather | solution.py:51
  2484.8 21.1 gather.24
  2505.8 20.1 select_reduce_fusion
  (38 shorter events, 0.3 us)
Async XLA Ops:
  7.2 313.7 %copy-start = (bf16[2048,512]{1,0:T(8,128)(2,1)S(1)}, bf16[2048,512]{1,0:T(8,128)(2,1)}, u32[]{:S(2)}) copy-start(bf16[2048,512]{1,0:T(8,128)(2,1)} %param.10) | copy-start | bytes 6291460
  8.5 33.2 %copy-start.2 = (s32[2048,6]{1,0:T(8,128)}, s32[2048,6]{1,0:T(8,128)S(1)}, u32[]{:S(2)}) copy-start(s32[2048,6]{1,0:T(8,128)S(1)} %copy.28) | copy-start | bytes 147460
  54.9 0.7 copy-start.4
  314.6 264.5 %all-to-all-start = ((f32[8,4640,1]{1,2,0:T(1,128)}), f32[8,4640,1]{1,2,0:T(1,128)}, u32[]{:S(2)}, u32[]{:S(2)}) async-start(f32[8,4640,1]{1,2,0:T(1,128)} %copy.34), calls=%async_computation | async-start | bytes 303104 | tf_op jit(solution)/shard_map/all_to_all | solution.py:73
  423.2 106.0 %copy-start.9 = (pred[37120]{0:T(1024)(128)(4,1)S(1)}, pred[37120]{0:T(1024)(128)(4,1)}, u32[]{:S(2)}) copy-start(pred[37120]{0:T(1024)(128)(4,1)} %get-tuple-element.20) | copy-start | bytes 111364
  1002.2 419.2 %all-to-all-start.2 = ((bf16[8,4640,512]{2,1,0:T(8,128)(2,1)}), bf16[8,4640,512]{2,1,0:T(8,128)(2,1)}, u32[]{:S(2)}, u32[]{:S(2)}) async-start(bf16[8,4640,512]{2,1,0:T(8,128)(2,1)} %bitcast.114), calls=%async_computation.2 | async-start | bytes 76021760 | tf_op jit(solution)/shard_map/all_to_all | solution.py:71
  1009.7 101.2 %all-gather.4.cloned.1.call-start = ((), (), s32[]{:S(2)}) async-start(), calls=%async_computation.8 | async-start | bytes 11796480 | tf_op jit(solution)/shard_map/all_gather | solution.py:76
  1010.4 199.2 %all-gather.6.cloned.1.call-start = ((), (), s32[]{:S(2)}) async-start(), calls=%async_computation.9 | async-start | bytes 11796480 | tf_op jit(solution)/shard_map/all_gather | solution.py:75
  1011.2 448.9 %all-gather.8.cloned.1.call-start = ((), (), s32[]{:S(2)}) async-start(), calls=%async_computation.10 | async-start | bytes 11796480 | tf_op jit(solution)/shard_map/all_gather | solution.py:74
  1011.9 1514.0 %reduce-scatter.8.cloned.1.call-start = ((), (), s32[]{:S(2)}) async-start(), calls=%async_computation.13 | async-start | bytes 23592960 | tf_op jit(solution)/shard_map/reduce_scatter | solution.py:86
  1013.4 137.9 %copy-start.7 = (f32[8,20,232]{2,1,0:T(8,128)}, f32[8,20,232]{2,1,0:T(8,128)S(1)}, u32[]{:S(2)}) copy-start(f32[8,20,232]{2,1,0:T(8,128)S(1)} %mul.65) | copy-start | bytes 445444
  1460.1 82.6 %copy-start.8 = (f32[8,20,232]{2,1,0:T(8,128)S(1)}, f32[8,20,232]{2,1,0:T(8,128)}, u32[]{:S(2)}) copy-start(f32[8,20,232]{2,1,0:T(8,128)} %copy-done.7) | copy-start | bytes 445444
  1575.6 950.3 %reduce-scatter.6.cloned.1.call-start = ((), (), s32[]{:S(2)}) async-start(), calls=%async_computation.12 | async-start | bytes 23592960 | tf_op jit(solution)/shard_map/reduce_scatter | solution.py:85
  1639.3 118.0 %all-to-all-start.4 = ((f32[8,4640,1]{1,2,0:T(1,128)}), f32[8,4640,1]{1,2,0:T(1,128)S(1)}, u32[]{:S(2)}, u32[]{:S(2)}) async-start(f32[8,4640,1]{1,2,0:T(1,128)} %all_to_all.43), calls=%async_computation.4 | async-start | bytes 303104 | tf_op jit(solution)/shard_map/all_to_all | solution.py:80
  1757.4 419.3 %all-to-all-start.3 = ((bf16[8,4640,512]{2,1,0:T(8,128)(2,1)}), bf16[8,4640,512]{2,1,0:T(8,128)(2,1)}, u32[]{:S(2)}, u32[]{:S(2)}) async-start(bf16[8,4640,512]{2,1,0:T(8,128)(2,1)} %bitcast.113), calls=%async_computation.3 | async-start | bytes 76021760 | tf_op jit(solution)/shard_map/all_to_all | solution.py:79
  1764.9 34.1 %copy-start.5 = (s32[12288]{0:T(1024)S(1)}, s32[12288]{0:T(1024)}, u32[]{:S(2)}) copy-start(s32[12288]{0:T(1024)} %copy-done.4) | copy-start | bytes 147460
  1764.9 35.2 %copy-start.6 = (s32[12288,1]{0,1:T(1,128)S(1)}, s32[12288,1]{0,1:T(1,128)}, u32[]{:S(2)}) copy-start(s32[12288,1]{0,1:T(1,128)} %get-tuple-element.18) | copy-start | bytes 147460
  1764.9 761.0 %reduce-scatter.4.cloned.1.call-start = ((), (), s32[]{:S(2)}) async-start(), calls=%async_computation.11 | async-start | bytes 23592960 | tf_op jit(solution)/shard_map/reduce_scatter | solution.py:84
  1799.0 71.6 %copy-start.3 = (s32[2048,6]{1,0:T(8,128)S(1)}, s32[2048,6]{1,0:T(8,128)}, u32[]{:S(2)}) copy-start(s32[2048,6]{1,0:T(8,128)} %copy-done.2) | copy-start | bytes 147460
  2176.6 349.3 %copy-start.1 = (bf16[2048,512]{1,0:T(8,128)(2,1)S(1)}, bf16[2048,512]{1,0:T(8,128)(2,1)}, u32[]{:S(2)}) copy-start(bf16[2048,512]{1,0:T(8,128)(2,1)} %param.10) | copy-start | bytes 6291460
Sparse Core Ops, SparseCore 0:
  1012.0 98.8 all-gather.3
  1112.4 97.1 all-gather.5
  1211.2 97.1 all-gather.7
  1575.7 176.0 reduce-scatter.7
  1754.6 176.4 reduce-scatter.5
  1933.8 176.4 reduce-scatter.3
where the time goes:
time: 2540 us; the launch traced here: 2530 us
  local copies, waits for them, and re-layouts  849 us (33%)
  waiting for transfers between devices  671 us (26%)
  blocking collectives  423 us (17%)
  matrix products  380 us (15%)
  other arithmetic  171 us (7%)
    gather x8, local copies, waits for them, and re-layouts, take_rows(): return jnp.take(rows, row_ids, axis=0, mode='fill', fill_value=0)  798 us
    all_to_all x1, blocking collectives, per_device(): lax.all_to_all(dy_send, 'ep', 0, 0, tiled=True)  423 us
    all_to_all x1, waiting for transfers between devices, per_device(): lax.all_to_all(dx_rows.reshape(n_ep * exp_local * capacity, d_model), 'ep...  301 us
    all_to_all x1, waiting for transfers between devices, per_device(): lax.all_to_all(x_send, 'ep', 0, 0, tiled=True)  212 us
    all_gather x1, waiting for transfers between devices, per_device(): w_down_full = lax.all_gather(w_down, 'fsdp', axis=2, tiled=True)  97.5 us
    dot_general x1, matrix products, expert_backward(): jnp.einsum('secd,edf->secf', x_rows, w_gate_full, preferred_element_type=...  82.6 us
    scatter-add x1, other arithmetic, route_slots(): jax.ops.segment_sum(jnp.arange(1, n_pairs + 1, dtype=jnp.int32), dest_slo...  64.5 us
    all_gather x1, waiting for transfers between devices, per_device(): w_up_full = lax.all_gather(w_up, 'fsdp', axis=1, tiled=True)  58.3 us
  transfers between devices with their start and end apart: 10, of which 4 were waited for; matrix products, arithmetic and copies ran while one was open for 39% of the time, Pallas kernels for 0%

commit v1 on v0

v1 whole, which is shorter than its diff:
```python
import functools

import jax
import jax.numpy as jnp
from jax import lax
from jax.experimental import pallas as pl
from jax.experimental.pallas import tpu as pltpu
from jax.sharding import PartitionSpec as P

CAP_FACTOR = 3
SUB = 16
BLK = 256
META = 128
F32 = jnp.float32
BF16 = jnp.bfloat16


def capacity_of(tok_dev, top_k, experts):
    return max(8, ((CAP_FACTOR * tok_dev * top_k // experts + 7) // 8) * 8)


def split3(v):
    hi = lax.reduce_precision(v, 8, 7)
    mid = lax.reduce_precision(v - hi, 8, 7)
    return hi, mid, v - hi - mid


def build_onehot(oh_ref, pos_ref, subexp, sublocal, first_sub):
    n_tok = oh_ref.shape[1]
    row_iota = lax.broadcasted_iota(jnp.int32, (SUB, n_tok), 0)
    for sub in range(BLK // SUB):
        q = first_sub + sub
        row = pos_ref[0, pl.ds(subexp[q], 1), :]
        hit = row_iota == (row - sublocal[q])
        oh_ref[sub * SUB:(sub + 1) * SUB, :] = jnp.where(hit, 1.0, 0.0).astype(BF16)


def gather_kernel(nsub_max, base, nblk, subexp, sublocal, subdst, half, xo, xp, do, dp, meta, pos, *rest):
    g_out, oh, buf, sem = rest[-4:]
    s = pl.program_id(0)
    k = base + s
    n = nblk[k]

    def wait(slot):
        pltpu.make_async_copy(buf.at[slot], g_out.at[pl.ds(0, BLK)], sem.at[slot]).wait()

    def block(b, _):
        slot = lax.rem(b, 2)
        first = k * nsub_max + b * (BLK // SUB)
        build_onehot(oh, pos, subexp, sublocal, first)

        @pl.when(b >= 2)
        def _():
            wait(slot)

        col = 0
        for ref in (xo, xp, do, dp, meta):
            w = ref.shape[1]
            buf[slot, :, col:col + w] = jnp.dot(oh[...], ref[...], preferred_element_type=F32).astype(BF16)
            col += w
        for sub in range(BLK // SUB):
            dst = pl.multiple_of(subdst[first + sub], SUB)
            pltpu.make_async_copy(buf.at[slot, pl.ds(sub * SUB, SUB)], g_out.at[pl.ds(dst, SUB)], sem.at[slot]).start()
        return 0

    lax.fori_loop(0, n, block, 0)

    @pl.when(n >= 1)
    def _():
        wait(lax.rem(n + 1, 2))

    @pl.when(n >= 2)
    def _():
        wait(lax.rem(n, 2))


def gather_call(base, tables, x_all, dy_all, meta_all, pos_all, rows, g_prev):
    nblk, subexp, sublocal, subdst, half = tables
    n_src = pos_all.shape[0]
    n_tok = pos_all.shape[2]
    nsub_max = subexp.shape[0] // nblk.shape[0]
    dh = x_all.shape[1] // 2
    width = 4 * dh + META
    own = pl.BlockSpec((n_tok, dh), lambda s, *t: (s, t[4][0]))
    oth = pl.BlockSpec((n_tok, dh), lambda s, *t: (s, 1 - t[4][0]))
    in_specs = [own, oth, own, oth,
                pl.BlockSpec((n_tok, META), lambda s, *t: (s, 0)),
                pl.BlockSpec((1,) + pos_all.shape[1:], lambda s, *t: (s, 0, 0))]
    args = [x_all, x_all, dy_all, dy_all, meta_all, pos_all]
    alias = {}
    if g_prev is not None:
        in_specs.append(pl.BlockSpec(memory_space=pl.ANY))
        args.append(g_prev)
        alias = {11: 0}
    return pl.pallas_call(
        functools.partial(gather_kernel, nsub_max, base),
        out_shape=jax.ShapeDtypeStruct((rows, width), BF16),
        grid_spec=pltpu.PrefetchScalarGridSpec(
            num_scalar_prefetch=5, grid=(n_src,), in_specs=in_specs,
            out_specs=pl.BlockSpec(memory_space=pl.ANY),
            scratch_shapes=[pltpu.VMEM((BLK, n_tok), BF16), pltpu.VMEM((2, BLK, width), BF16),
                            pltpu.SemaphoreType.DMA((2,))]),
        input_output_aliases=alias,
        cost_estimate=pl.CostEstimate(flops=int(40e9), bytes_accessed=int(60e6), transcendentals=0),
        name="gather_rows",
    )(nblk, subexp, sublocal, subdst, half, *args)


def nt_dot(a, b):
    return lax.dot_general(a, b, (((1,), (1,)), ((), ())), preferred_element_type=F32)


def tn_dot(a, b):
    return lax.dot_general(a, b, (((0,), (0,)), ((), ())), preferred_element_type=F32)


def expert_kernel(blk_end, exp_rows, first_expert, g_hbm, w1o, w1p, w3o, w3p, w2o, w2p, dx_hbm, dw1, dw3, dw2,
                  w13, w2, gbuf, dxbuf, gsem, dxsem):
    e = pl.program_id(0)
    dh = w1o.shape[1]
    d = 2 * dh
    f = w1o.shape[2]
    last = pl.num_programs(0) - 1
    total = blk_end[last]
    begin = jnp.where(e == 0, 0, blk_end[jnp.maximum(e - 1, 0)])
    end = blk_end[e]

    def fetch(b):
        src = pl.multiple_of(b * BLK, BLK)
        slot = lax.rem(b, 2)
        return pltpu.make_async_copy(g_hbm.at[pl.ds(src, BLK)], gbuf.at[slot], gsem.at[slot])

    def store(b):
        dst = pl.multiple_of(b * BLK, BLK)
        slot = lax.rem(b, 2)
        return pltpu.make_async_copy(dxbuf.at[slot], dx_hbm.at[pl.ds(dst, BLK)], dxsem.at[slot])

    @pl.when(e == 0)
    def _():
        fetch(0).start()

    w13[0:dh, 0:f] = w1o[0]
    w13[dh:d, 0:f] = w1p[0]
    w13[0:dh, f:2 * f] = w3o[0]
    w13[dh:d, f:2 * f] = w3p[0]
    w2[:, 0:dh] = w2o[0]
    w2[:, dh:d] = w2p[0]
    dw1[...] = jnp.zeros_like(dw1)
    dw3[...] = jnp.zeros_like(dw3)
    dw2[...] = jnp.zeros_like(dw2)

    def block(b, _):
        slot = lax.rem(b, 2)

        @pl.when(b + 1 < total)
        def _():
            fetch(b + 1).start()

        fetch(b).wait()

        @pl.when(b >= 2)
        def _():
            store(b - 2).wait()

        g = gbuf.at[slot]
        dx = dxbuf.at[slot]
        cnt = exp_rows[e] - (b - begin) * BLK

        def masked(v):
            keep = lax.broadcasted_iota(jnp.int32, v.shape, 0) < cnt
            return jnp.where(keep, v, jnp.zeros_like(v))

        x = masked(g[:, 0:d])
        dy = masked(g[:, d:2 * d])
        meta = masked(g[:, 2 * d:2 * d + META].astype(F32))
        lane = lax.broadcasted_iota(jnp.int32, meta.shape, 1)
        ids = pltpu.roll(meta, META - 32, 1)
        mine = (ids == (first_expert[0] + e).astype(F32)) & (lane < 24)

        def piece(c):
            return jnp.sum(jnp.where(mine & (lane >= 8 * c) & (lane < 8 * c + 8), meta, 0.0), axis=1, keepdims=True)

        r = piece(0) + piece(1) + piece(2)
        dy32 = dy.astype(F32)
        scaled = (r * dy32).astype(BF16)
        h = jnp.dot(x, w13[...], preferred_element_type=F32)
        h1 = h[:, :f]
        h3 = h[:, f:]
        sig = jax.nn.sigmoid(h1)
        act = ((h1 * sig) * h3).astype(BF16)
        y = jnp.dot(act, w2[:, 0:dh], preferred_element_type=F32)
        dr = jnp.sum(dy32[:, 0:dh] * y, axis=1, keepdims=True)
        da = nt_dot(scaled, w2[...])
        dh1 = (da * h3 * sig * (1.0 + h1 * (1.0 - sig))).astype(BF16)
        dh3 = (da * h1 * sig).astype(BF16)
        dx[:, 0:dh] = (nt_dot(dh1, w1o[0]) + nt_dot(dh3, w3o[0])).astype(BF16)
        hi = dr.astype(BF16).astype(F32)
        mid = (dr - hi).astype(BF16).astype(F32)
        lo = dr - hi - mid
        spread = jnp.where(lane < 8, hi, jnp.where(lane < 16, mid, lo))
        dx[:, dh:dh + META] = jnp.where(mine, spread, 0.0).astype(BF16)
        store(b).start()
        dw1[0] += tn_dot(x[:, 0:dh], dh1)
        dw3[0] += tn_dot(x[:, 0:dh], dh3)
        dw2[0] += tn_dot(act, scaled[:, 0:dh])
        return 0

    lax.fori_loop(begin, end, block, 0)

    @pl.when(e == last)
    def _():
        store(total - 1).wait()
        store(total - 2).wait()


def expert_call(blk_end, exp_rows, first_expert, g, w_own, w_oth, rows):
    e, dh, f = w_own[0].shape
    width = g.shape[1]
    wspec = pl.BlockSpec((1, dh, f), lambda e, *t: (e, 0, 0))
    dspec = pl.BlockSpec((1, f, dh), lambda e, *t: (e, 0, 0))
    hbm = pl.BlockSpec(memory_space=pl.ANY)
    return pl.pallas_call(
        expert_kernel,
        out_shape=(jax.ShapeDtypeStruct((rows, dh + META), BF16),
                   jax.ShapeDtypeStruct((e, dh, f), F32), jax.ShapeDtypeStruct((e, dh, f), F32),
                   jax.ShapeDtypeStruct((e, f, dh), F32)),
        grid_spec=pltpu.PrefetchScalarGridSpec(
            num_scalar_prefetch=3, grid=(e,),
            in_specs=[hbm, wspec, wspec, wspec, wspec, dspec, dspec],
            out_specs=[hbm, wspec, wspec, dspec],
            scratch_shapes=[pltpu.VMEM((2 * dh, 2 * f), BF16), pltpu.VMEM((f, 2 * dh), BF16),
                            pltpu.VMEM((2, BLK, width), BF16), pltpu.VMEM((2, BLK, dh + META), BF16),
                            pltpu.SemaphoreType.DMA((2,)), pltpu.SemaphoreType.DMA((2,))]),
        cost_estimate=pl.CostEstimate(flops=int(60e9), bytes_accessed=int(120e6), transcendentals=0),
        name="expert_backward",
    )(blk_end, exp_rows, first_expert, g, w_own[0], w_oth[0], w_own[1], w_oth[1], w_own[2], w_oth[2])


def scatter_kernel(nsub_max, base, dh, nblk, subexp, sublocal, subsrc, pos, dx_hbm, out, oh, buf, dracc, sem):
    s = pl.program_id(0)
    k = base + s
    n = nblk[k]
    out[...] = jnp.zeros_like(out)
    dracc[...] = jnp.zeros_like(dracc)

    def fetch(b, slot):
        first = k * nsub_max + b * (BLK // SUB)
        for sub in range(BLK // SUB):
            src = pl.multiple_of(subsrc[first + sub], SUB)
            pltpu.make_async_copy(dx_hbm.at[pl.ds(src, SUB)], buf.at[slot, pl.ds(sub * SUB, SUB)], sem.at[slot]).start()

    @pl.when(n >= 1)
    def _():
        fetch(0, 0)

    def block(b, _):
        slot = lax.rem(b, 2)

        @pl.when(b + 1 < n)
        def _():
            fetch(b + 1, 1 - slot)

        build_onehot(oh, pos, subexp, sublocal, k * nsub_max + b * (BLK // SUB))
        pltpu.make_async_copy(dx_hbm.at[pl.ds(0, BLK)], buf.at[slot], sem.at[slot]).wait()
        out[0, 0:dh, :] += tn_dot(buf[slot, :, 0:dh], oh[...])
        dracc[...] += tn_dot(buf[slot, :, dh:dh + META], oh[...])
        return 0

    lax.fori_loop(0, n, block, 0)
    out[0, dh:dh + 8, :] = dracc[0:8, :] + dracc[8:16, :] + dracc[16:24, :]


def scatter_call(base, nblk, subexp, sublocal, subsrc, pos_all, dx_rows):
    n_src, _, n_tok = pos_all.shape
    dh = dx_rows.shape[1] - META
    nsub_max = subexp.shape[0] // nblk.shape[0]
    return pl.pallas_call(
        functools.partial(scatter_kernel, nsub_max, base, dh),
        out_shape=jax.ShapeDtypeStruct((n_src, dh + 8, n_tok), F32),
        grid_spec=pltpu.PrefetchScalarGridSpec(
            num_scalar_prefetch=4, grid=(n_src,),
            in_specs=[pl.BlockSpec((1,) + pos_all.shape[1:], lambda s, *t: (s, 0, 0)),
                      pl.BlockSpec(memory_space=pl.ANY)],
            out_specs=pl.BlockSpec((1, dh + 8, n_tok), lambda s, *t: (s, 0, 0)),
            scratch_shapes=[pltpu.VMEM((BLK, n_tok), BF16), pltpu.VMEM((2, BLK, dh + META), BF16),
                            pltpu.VMEM((META, n_tok), F32), pltpu.SemaphoreType.DMA((2,))]),
        cost_estimate=pl.CostEstimate(flops=int(10e9), bytes_accessed=int(30e6), transcendentals=0),
        name="scatter_rows",
    )(nblk, subexp, sublocal, subsrc, pos_all, dx_rows)


def routing_tables(ids, first_expert, n_exp, capacity):
    n_src, _, n_tok = ids.shape
    eid = first_expert.astype(F32) + jnp.arange(n_exp, dtype=F32)
    mask = jnp.any(ids[:, None, :, :] == eid[None, :, None, None], axis=2)
    upper = (jnp.arange(n_tok)[:, None] < jnp.arange(n_tok)[None, :]).astype(BF16)
    before = jnp.dot(mask.reshape(n_src * n_exp, n_tok).astype(BF16), upper, preferred_element_type=F32)
    before = before.reshape(n_src, n_exp, n_tok)
    kept = mask & (before < capacity)
    pos = jnp.where(kept, before, -1.0).astype(jnp.int32)
    pos = jnp.pad(pos, ((0, 0), (0, (-n_exp) % 8), (0, 0)), constant_values=-1)
    cnt = jnp.sum(kept.astype(jnp.int32), axis=2)
    subs = (cnt + SUB - 1) // SUB
    cap_subs = -(-capacity // SUB)
    nsub_max = -(-n_exp * cap_subs // (BLK // SUB)) * (BLK // SUB)
    src_end = jnp.cumsum(subs, axis=1)
    src_off = src_end - subs
    nsub = src_end[:, -1]
    exp_subs = jnp.sum(subs, axis=0)
    exp_blocks = jnp.maximum(1, -(-exp_subs // (BLK // SUB)))
    blk_end = jnp.cumsum(exp_blocks)
    blk_off = blk_end - exp_blocks
    seg_off = blk_off[None, :] * (BLK // SUB) + jnp.cumsum(subs, axis=0) - subs
    q = jnp.arange(nsub_max, dtype=jnp.int32)
    subexp = jnp.minimum(jnp.sum((src_end[:, None, :] <= q[None, :, None]).astype(jnp.int32), axis=2), n_exp - 1)
    pick = subexp[:, :, None] == jnp.arange(n_exp)[None, None, :]
    rel = q[None, :] - jnp.sum(jnp.where(pick, src_off[:, None, :], 0), axis=2)
    live = q[None, :] < nsub[:, None]
    sublocal = jnp.where(live, rel * SUB, 1 << 20)
    seg = jnp.sum(jnp.where(pick, seg_off[:, None, :], 0), axis=2) + rel
    max_blocks = n_exp * max(1, -(-n_src * cap_subs // (BLK // SUB)))
    rows = max_blocks * BLK
    spare = rows + (q % (BLK // SUB))[None, :] * SUB
    subdst = jnp.where(live, seg * SUB, spare)
    subsrc = jnp.where(live, seg * SUB, 0)
    nblk = -(-nsub // (BLK // SUB))
    return (pos, nblk, subexp.reshape(-1), sublocal.reshape(-1), subdst.reshape(-1), subsrc.reshape(-1),
            blk_end, exp_subs * SUB, rows)


def solution(mesh):
    n_ep = mesh.shape["ep"]
    tok_spec = P(("fsdp", "ep"), None)
    spec_in = P("ep", "fsdp", None)
    spec_out = P("ep", None, "fsdp")
    swap = [(0, 1), (1, 0)]

    def per_device(x_tok, dy_tok, expert_ids, route_w, w_gate, w_up, w_down):
        tok_dev, top_k = expert_ids.shape
        exp_local = w_gate.shape[0]
        dh = w_gate.shape[1]
        capacity = capacity_of(tok_dev, top_k, exp_local * n_ep)
        me = lax.axis_index("fsdp")
        pad = ((0, 8 - top_k), (0, 0))
        info = jnp.stack([jnp.pad(expert_ids.T.astype(F32), pad, constant_values=-1.0),
                          jnp.pad(route_w.T, pad)])
        info = lax.all_gather(info, ("fsdp", "ep"), axis=0, tiled=False)
        info = info.reshape(2, n_ep, 2, 8, tok_dev)
        x_z = lax.ppermute(x_tok, "fsdp", swap)
        dy_z = lax.ppermute(dy_tok, "fsdp", swap)
        w_own = (w_gate, w_up, w_down)
        w_oth = tuple(lax.ppermute(w, "fsdp", swap) for w in w_own)
        x_a = lax.all_gather(x_tok, "ep", axis=0, tiled=True)
        dy_a = lax.all_gather(dy_tok, "ep", axis=0, tiled=True)
        x_b = lax.all_gather(x_z, "ep", axis=0, tiled=True)
        dy_b = lax.all_gather(dy_z, "ep", axis=0, tiled=True)

        info = jnp.where(me == 0, info, info[::-1]).reshape(2 * n_ep, 2, 8, tok_dev)
        ids = info[:, 0]
        first_expert = lax.axis_index("ep") * exp_local
        (pos, nblk, subexp, sublocal, subdst, subsrc, blk_end, exp_rows, rows) = routing_tables(
            ids, first_expert, exp_local, capacity)
        hi, mid, lo = split3(info[:, 1])
        none = jnp.zeros_like(hi)
        meta = jnp.concatenate([hi, mid, lo, none, ids, ids, ids] + [none] * 9, axis=1)
        meta = meta.astype(BF16).transpose(0, 2, 1).reshape(2, n_ep * tok_dev, META)
        half = me.reshape(1)
        tables = (nblk, subexp, sublocal, subdst, half)
        g = gather_call(0, tables, x_a, dy_a, meta[0], pos[:n_ep], rows + BLK, None)
        g = gather_call(n_ep, tables, x_b, dy_b, meta[1], pos[n_ep:], rows + BLK, g)
        dx_rows, dw_gate, dw_up, dw_down = expert_call(
            blk_end, exp_rows, first_expert.reshape(1), g, w_own, w_oth, rows)
        out_a = scatter_call(0, nblk, subexp, sublocal, subsrc, pos[:n_ep], dx_rows)
        out_b = scatter_call(n_ep, nblk, subexp, sublocal, subsrc, pos[n_ep:], dx_rows)
        sum_b = lax.psum_scatter(out_b, "ep", scatter_dimension=0, tiled=False)
        sum_a = lax.psum_scatter(out_a, "ep", scatter_dimension=0, tiled=False)
        dx_other = lax.ppermute(sum_b[:dh].astype(BF16), "fsdp", swap)
        dr_other = lax.ppermute(sum_b[dh:], "fsdp", swap)
        dx_mine = sum_a[:dh].astype(BF16)
        grad_x = jnp.where(me == 0, jnp.concatenate([dx_mine, dx_other]), jnp.concatenate([dx_other, dx_mine])).T
        route_grad = (sum_a[dh:] + dr_other)[:top_k].T
        return grad_x, route_grad, dw_gate, dw_up, dw_down

    return jax.shard_map(
        per_device, mesh=mesh,
        in_specs=(tok_spec, tok_spec, tok_spec, tok_spec, spec_in, spec_in, spec_out),
        out_specs=(tok_spec, tok_spec, spec_in, spec_in, spec_out),
        check_vma=False)
```

time: 2540 us -> 925 us (0.36)
  local copies, waits for them, and re-layouts: 849 us -> 117 us
  blocking collectives: 423 us -> 0 us
  Pallas kernels: 0 us -> 376 us
  matrix products: 380 us -> 5.29 us
  waiting for transfers between devices: 671 us -> 380 us
  other arithmetic: 171 us -> 19.7 us
    gather x8 -> x0, local copies, waits for them, and re-layouts: 798 us -> none  [take_rows(): return jnp.take(rows, row_ids, axis=0, mode='fill', fill_value=0)]
    all_to_all x4 -> x0, waiting for transfers between devices: 513 us -> none  [the longest x1 301 us: per_device(): lax.all_to_all(dx_rows.reshape(n_ep * exp_local * capacity, d_model), 'ep...]
    all_to_all x1 -> x0, blocking collectives: 423 us -> none  [per_device(): lax.all_to_all(dy_send, 'ep', 0, 0, tiled=True)]
    pallas_call x0 -> x5, Pallas kernels: none -> 376 us  [the longest x2 159 us: gather_call(): pl.pallas_call(functools.partial(gather_kernel, nsub_max, base), out_shap...]
    dot_general x9 -> x1, matrix products: 380 us -> 5.29 us  [routing_tables(): jnp.dot(mask.reshape(n_src * n_exp, n_tok).astype(BF16), upper, preferred...]
    reduce_scatter x3 -> x2, waiting for transfers between devices: 0.01 us -> 206 us  [the longest x1 111 us: per_device(): sum_a = lax.psum_scatter(out_a, 'ep', scatter_dimension=0, tiled=False)]
    ppermute x0 -> x7, waiting for transfers between devices: none -> 97.4 us  [the longest x1 52.2 us: per_device(): x_z = lax.ppermute(x_tok, 'fsdp', swap)]
    all_gather x3 -> x5, waiting for transfers between devices: 156 us -> 75.6 us  [the longest x1 75.5 us: per_device(): dy_b = lax.all_gather(dy_z, 'ep', axis=0, tiled=True)]
  transfers between devices with their start and end apart: 10 -> 14, of which waited for: 4 -> 5; matrix products, arithmetic and copies ran while one was open for 39% -> 15% of each run, Pallas kernels for 0% -> 23%
where the time goes in v1:
time: 925 us; the launch traced here: 923 us
  waiting for transfers between devices  380 us (41%)
  Pallas kernels  376 us (41%)
  local copies, waits for them, and re-layouts  117 us (13%)
  other arithmetic  19.7 us (2%)
  between operations  14.3 us (2%)
  starting transfers between devices  11 us (1%)
    pallas_call x2, Pallas kernels, gather_call(): pl.pallas_call(functools.partial(gather_kernel, nsub_max, base), out_shap...  159 us
    pallas_call x1, Pallas kernels, expert_call(): pl.pallas_call(expert_kernel, out_shape=(jax.ShapeDtypeStruct((rows, dh +...  114 us
    reduce_scatter x1, waiting for transfers between devices, per_device(): sum_a = lax.psum_scatter(out_a, 'ep', scatter_dimension=0, tiled=False)  111 us
    pallas_call x2, Pallas kernels, scatter_call(): pl.pallas_call(functools.partial(scatter_kernel, nsub_max, base, dh), out...  102 us
    reduce_scatter x1, waiting for transfers between devices, per_device(): sum_b = lax.psum_scatter(out_b, 'ep', scatter_dimension=0, tiled=False)  94.4 us
    all_gather x1, waiting for transfers between devices, per_device(): dy_b = lax.all_gather(dy_z, 'ep', axis=0, tiled=True)  75.5 us
    concatenate x2, local copies, waits for them, and re-layouts, per_device(): jnp.concatenate([hi, mid, lo, none, ids, ids, ids] + [none] * 9, axis=1)  65.3 us
    ppermute x1, waiting for transfers between devices, per_device(): x_z = lax.ppermute(x_tok, 'fsdp', swap)  52.2 us
  transfers between devices with their start and end apart: 14, of which 5 were waited for; matrix products, arithmetic and copies ran while one was open for 15% of the time, Pallas kernels for 23%

profile of v1, /device:TPU:0, one launch (start us, length us, event | category | flops | bytes accessed | tf_op | source)
XLA Modules:
  0.0 922.6 jit_solution(823007730950258909)
XLA Ops:
  7.2 1.0 convert_bitcast_fusion
  8.2 0.9 pad_bitcast_fusion
  9.1 0.7 pad_maximum_fusion
  9.8 0.7 all-gather.11.cloned.1.call-update
  10.6 0.7 all-gather.13.cloned.1.call-update
  11.3 3.3 collective-permute-start
  14.6 52.2 %collective-permute-done = bf16[2048,512]{1,0:T(8,128)(2,1)} collective-permute-done((bf16[2048,512]{1,0:T(8,128)(2,1)S(1)}, bf16[2048,512]{1,0:T(8,128)(2,1)}, u32[]{:S(2)}, u32[]{:S(2)}) %collective-permute-start) | collective-permute-done | bytes 2097184 | tf_op jit(solution)/shard_map/ppermute | solution.py:349
  66.9 1.8 collective-permute-start.1
  68.7 45.2 %collective-permute-done.1 = bf16[2048,512]{1,0:T(8,128)(2,1)S(1)} collective-permute-done((bf16[2048,512]{1,0:T(8,128)(2,1)}, bf16[2048,512]{1,0:T(8,128)(2,1)S(1)}, u32[]{:S(2)}, u32[]{:S(2)}) %collective-permute-start.1) | collective-permute-done | bytes 2097184 | tf_op jit(solution)/shard_map/ppermute | solution.py:350
  113.9 1.3 copy-done.2
  115.3 1.5 collective-permute-start.2
  116.8 0.6 collective-permute-start.3
  117.3 1.5 collective-permute-start.4
  118.8 1.7 copy.33
  120.6 0.3 reverse_select_fusion
  120.8 0.1 slice_bitcast_fusion.1
  120.9 9.4 %compare_reduce_fusion = pred[16,20,2048]{2,1,0:T(8,128)(4,1)S(1)} fusion(f32[16,8,2048]{2,1,0:T(8,128)S(1)} %slice_bitcast_fusion.1, f32[20]{0:T(128)S(1)} %iota_add_fusion), kind=kLoop, calls=%fused_computation | loop fusion | flops 9830400 | bytes 1704016 | tf_op jit(solution)/shard_map/reduce_or | solution.py:295
  130.3 5.3 fusion.5
  135.6 0.8 convert_reduce_fusion
  136.4 0.2 reduce_window_sum.29
  136.6 0.1 copy.34
  136.7 0.1 convert_reduce_fusion.1
  136.8 0.7 min.16.subexp
  137.5 0.1 copy.36
  137.7 0.1 reduce.1.blk_end
  137.8 0.5 broadcast_multiply_fusion
  138.3 0.1 copy.37
  138.4 0.1 copy.35
  138.5 0.2 slice_reduce_fusion
  138.7 0.2 select_reduce_fusion
  138.8 0.1 fusion.10
  138.9 0.7 select_n.107.sublocal
  139.6 0.7 select_n.112.subsrc
  140.3 0.7 select_n.116.subdst
  141.0 1.2 fusion.6
  142.2 7.2 copy.38
  149.4 7.1 copy.39
  156.5 5.8 copy.40
  162.3 0.1 fusion.20
  162.4 5.7 copy.41
  168.1 4.8 broadcast_in_dim.60
  172.9 4.8 concatenate.13
  177.8 60.5 %concatenate.14 = bf16[16,128,2048]{1,2,0:T(8,128)(2,1)} concatenate(bf16[16,8,2048]{1,2,0:T(8,128)(2,1)} %copy.38, bf16[16,8,2048]{1,2,0:T(8,128)(2,1)} %copy.39, bf16[16,8,2048]{1,2,0:T(8,128)(2,1)} %copy.40, bf16[16,8,2048]{1,2,0:T(8,128)(2,1)} %broadcast_in_dim.60, bf16[16,8,2048]{1,2,0:T(8,128)(2,1)} %copy.41, bf16[16,8,2048]{1,2,0:T(8,128)(2,1)} %copy.41, ...), dimensions={1} | concatenate | bytes 16777216 | tf_op jit(solution)/shard_map/concatenate | solution.py:365
  238.3 0.5 fusion.19.nblk
  238.8 3.0 select_convert_fusion
  241.8 2.0 pad_slice_fusion.1
  243.8 3.6 fusion.22
  247.4 77.8 %gather_rows.2.rest_0_ = bf16[77056,1152]{1,0:T(8,128)(2,1)} custom-call(s32[16]{0:T(128)} %fusion.19.nblk, s32[4864]{0:T(1024)} %min.16.subexp, s32[4864]{0:T(1024)} %select_n.107.sublocal, s32[4864]{0:T(1024)} %select_n.116.subdst, s32[1]{0:T(128)} %bitcast.10.half, bf16[16384,512]{1,0:T(8,128)(2,1)} %all-gather.11.cloned.1.call-done.xo.xp, ...), custom_call_target="tpu_custom_call" | custom-call | flops 40000000000 | bytes 60000000 | tf_op jit(solution)/shard_map/gather_rows/pallas_call | solution.py:95
  325.3 75.5 %all-gather.9.cloned.1.call-done.do.dp = bf16[16384,512]{1,0:T(8,128)(2,1)} async-done(((bf16[2048,512]{1,0:T(8,128)(2,1)}), bf16[16384,512]{1,0:T(8,128)(2,1)}) %all-gather.9.cloned.1.call-update) | async-done | bytes 16777232 | tf_op jit(solution)/shard_map/all_gather | solution.py:356
  400.8 81.5 %gather_rows.3.g_hbm = bf16[77056,1152]{1,0:T(8,128)(2,1)} custom-call(s32[16]{0:T(128)} %fusion.19.nblk, s32[4864]{0:T(1024)} %min.16.subexp, s32[4864]{0:T(1024)} %select_n.107.sublocal, s32[4864]{0:T(1024)} %select_n.116.subdst, s32[1]{0:T(128)} %bitcast.10.half, ...), custom_call_target="tpu_custom_call", output_to_operand_aliasing={{}: (11, {})} | custom-call | flops 40000000000 | bytes 60000000 | tf_op jit(solution)/shard_map/gather_rows/pallas_call | solution.py:95
  482.4 114.0 %expert_backward.1 = (bf16[76800,384]{1,0:T(8,128)(2,1)}, f32[20,256,384]{2,1,0:T(8,128)}, f32[20,256,384]{2,1,0:T(8,128)}, f32[20,384,256]{2,1,0:T(8,128)}) custom-call(s32[20]{0:T(128)} %copy-done.3, s32[20]{0:T(128)} %get-tuple-element.54.exp_rows, s32[1]{0:T(128)} %bitcast.9.first_expert, bf16[77056,1152]{1,0:T(8,128)(2,1)} %gather_rows.3.g_hbm, ...), custom_call_target="tpu_custom_call" | custom-call | flops 60000002048 | bytes 120000000 | tf_op jit(solution)/shard_map/expert_backward/pallas_call | solution.py:222
  596.3 52.0 %scatter_rows.3 = f32[8,264,2048]{2,1,0:T(8,128)} custom-call(s32[16]{0:T(128)} %fusion.19.nblk, s32[4864]{0:T(1024)} %min.16.subexp, s32[4864]{0:T(1024)} %select_n.107.sublocal, s32[4864]{0:T(1024)} %select_n.112.subsrc, s32[8,24,2048]{2,1,0:T(8,128)} %get-tuple-element.45.pos, bf16[76800,384]{1,0:T(8,128)(2,1)} %get-tuple-element.9.dx_hbm), custom_call_target="tpu_custom_call" | custom-call | flops 10000000000 | bytes 30000000 | tf_op jit(solution)/shard_map/scatter_rows/pallas_call | solution.py:277
  648.4 50.3 %scatter_rows.2 = f32[8,264,2048]{2,1,0:T(8,128)} custom-call(s32[16]{0:T(128)} %fusion.19.nblk, s32[4864]{0:T(1024)} %min.16.subexp, s32[4864]{0:T(1024)} %select_n.107.sublocal, s32[4864]{0:T(1024)} %select_n.112.subsrc, s32[8,24,2048]{2,1,0:T(8,128)} %get-tuple-element.44.pos, bf16[76800,384]{1,0:T(8,128)(2,1)} %get-tuple-element.9.dx_hbm), custom_call_target="tpu_custom_call" | custom-call | flops 10000000000 | bytes 30000000 | tf_op jit(solution)/shard_map/scatter_rows/pallas_call | solution.py:277
  698.7 94.4 %reduce-scatter.5.cloned.1.call-done = f32[1,264,2048]{2,1,0:T(8,128)} async-done(((f32[8,264,2048]{2,1,0:T(8,128)}), f32[1,264,2048]{2,1,0:T(8,128)}) %reduce-scatter.5.cloned.1.call-update) | async-done | bytes 2162704 | tf_op jit(solution)/shard_map/reduce_scatter | solution.py:375
  793.1 1.7 fusion.8
  794.8 1.5 collective-permute-start.5
  796.3 0.8 slice_bitcast_fusion.2
  797.2 0.5 collective-permute-start.6
  797.7 111.3 %reduce-scatter.3.cloned.1.call-done = f32[1,264,2048]{2,1,0:T(8,128)} async-done(((f32[8,264,2048]{2,1,0:T(8,128)}), f32[1,264,2048]{2,1,0:T(8,128)}) %reduce-scatter.3.cloned.1.call-update) | async-done | bytes 2162704 | tf_op jit(solution)/shard_map/reduce_scatter | solution.py:376
  909.0 1.7 fusion.7
  910.8 0.8 slice_bitcast_fusion.3
  911.6 0.6 fusion.9
  912.2 1.0 fusion.4
  913.2 2.5 copy.44
  (36 shorter events, 0.6 us)
Async XLA Ops:
  7.2 4.1 copy-start.1
  7.2 111.6 %all-gather.15.cloned.1.call-start = ((), (), s32[]{:S(2)}) async-start(), calls=%async_computation.8 | async-start | bytes 2228224 | tf_op jit(solution)/shard_map/all_gather | solution.py:347
  9.8 237.7 %all-gather.11.cloned.1.call-start = ((), (), s32[]{:S(2)}) async-start(), calls=%async_computation.4 | async-start | bytes 18874368 | tf_op jit(solution)/shard_map/all_gather | solution.py:353
  10.5 236.9 %all-gather.13.cloned.1.call-start = ((), (), s32[]{:S(2)}) async-start(), calls=%async_computation.5 | async-start | bytes 18874368 | tf_op jit(solution)/shard_map/all_gather | solution.py:354
  11.2 314.0 %all-gather.7.cloned.1.call-start = ((), (), s32[]{:S(2)}) async-start(), calls=%async_computation.2 | async-start | bytes 18874368 | tf_op jit(solution)/shard_map/all_gather | solution.py:355
  11.3 55.6 %collective-permute-start = (bf16[2048,512]{1,0:T(8,128)(2,1)S(1)}, bf16[2048,512]{1,0:T(8,128)(2,1)}, u32[]{:S(2)}, u32[]{:S(2)}) collective-permute-start(bf16[2048,512]{1,0:T(8,128)(2,1)S(1)} %copy-done.1), channel_id=1, source_target_pairs={{0,8},{8,0},{1,9},{9,1},{2,10},{10,2},{3,11},{11,3},{4,12},{12,4},... | collective-permute-start | bytes 6291464 | tf_op jit(solution)/shard_map/ppermute | solution.py:349
  66.9 333.9 %all-gather.9.cloned.1.call-start = ((), (), s32[]{:S(2)}) async-start(), calls=%async_computation.3 | async-start | bytes 18874368 | tf_op jit(solution)/shard_map/all_gather | solution.py:356
  66.9 46.9 %collective-permute-start.1 = (bf16[2048,512]{1,0:T(8,128)(2,1)}, bf16[2048,512]{1,0:T(8,128)(2,1)S(1)}, u32[]{:S(2)}, u32[]{:S(2)}) collective-permute-start(bf16[2048,512]{1,0:T(8,128)(2,1)} %param.8), channel_id=1, source_target_pairs={{0,8},{8,0},{1,9},{9,1},{2,10},{10,2},{3,11},{11,3},{4,12},{12,4},... | collective-permute-start | bytes 6291464 | tf_op jit(solution)/shard_map/ppermute | solution.py:350
  113.9 1.3 copy-start.2
  115.2 677.9 %reduce-scatter.5.cloned.1.call-start = ((), (), s32[]{:S(2)}) async-start(), calls=%async_computation.7 | async-start | bytes 19464192 | tf_op jit(solution)/shard_map/reduce_scatter | solution.py:375
  115.3 367.1 %collective-permute-start.2 = (bf16[20,256,384]{2,1,0:T(8,128)(2,1)}, bf16[20,256,384]{2,1,0:T(8,128)(2,1)}, u32[]{:S(2)}, u32[]{:S(2)}) collective-permute-start(bf16[20,256,384]{2,1,0:T(8,128)(2,1)} %w1o.1), channel_id=1, source_target_pairs={{0,8},{8,0},{1,9},{9,1},{2,10},{10,2},{3,11},{11,3},{4,12},{12,4},... | collective-permute-start | bytes 11796488 | tf_op jit(solution)/shard_map/ppermute | solution.py:352
  116.8 365.6 %collective-permute-start.3 = (bf16[20,256,384]{2,1,0:T(8,128)(2,1)}, bf16[20,256,384]{2,1,0:T(8,128)(2,1)}, u32[]{:S(2)}, u32[]{:S(2)}) collective-permute-start(bf16[20,256,384]{2,1,0:T(8,128)(2,1)} %w3o.1), channel_id=1, source_target_pairs={{0,8},{8,0},{1,9},{9,1},{2,10},{10,2},{3,11},{11,3},{4,12},{12,4},... | collective-permute-start | bytes 11796488 | tf_op jit(solution)/shard_map/ppermute | solution.py:352
  117.3 365.0 %collective-permute-start.4 = (bf16[20,384,256]{2,1,0:T(8,128)(2,1)}, bf16[20,384,256]{2,1,0:T(8,128)(2,1)}, u32[]{:S(2)}, u32[]{:S(2)}) collective-permute-start(bf16[20,384,256]{2,1,0:T(8,128)(2,1)} %w2o.1), channel_id=1, source_target_pairs={{0,8},{8,0},{1,9},{9,1},{2,10},{10,2},{3,11},{11,3},{4,12},{12,4},... | collective-permute-start | bytes 11796488 | tf_op jit(solution)/shard_map/ppermute | solution.py:352
  137.8 0.5 copy-start.3
  238.8 5.0 copy-start
  648.4 260.6 %reduce-scatter.3.cloned.1.call-start = ((), (), s32[]{:S(2)}) async-start(), calls=%async_computation.6 | async-start | bytes 19464192 | tf_op jit(solution)/shard_map/reduce_scatter | solution.py:376
  794.8 117.4 %collective-permute-start.5 = (bf16[256,2048]{1,0:T(8,128)(2,1)S(1)}, bf16[256,2048]{1,0:T(8,128)(2,1)S(1)}, u32[]{:S(2)}, u32[]{:S(2)}) collective-permute-start(bf16[256,2048]{1,0:T(8,128)(2,1)S(1)} %fusion.8), channel_id=1, source_target_pairs={{0,8},{8,0},{1,9},{9,1},{2,10},{10,2},{3,11},{11,3},{4,12},{12,4},... | collective-permute-start | bytes 3145736 | tf_op jit(solution)/shard_map/ppermute | solution.py:377
  797.2 114.4 %collective-permute-start.6 = (f32[8,2048]{1,0:T(8,128)S(1)}, f32[8,2048]{1,0:T(8,128)S(1)}, u32[]{:S(2)}, u32[]{:S(2)}) collective-permute-start(f32[8,2048]{1,0:T(8,128)S(1)} %slice_bitcast_fusion.2), channel_id=1, source_target_pairs={{0,8},{8,0},{1,9},{9,1},{2,10},{10,2},{3,11},{11,3},{4,12},{12,4},... | collective-permute-start | bytes 196616 | tf_op jit(solution)/shard_map/ppermute | solution.py:378
Sparse Core Ops, SparseCore 0:
  10.8 38.6 all-gather.14
  51.3 85.8 all-gather.10
  139.1 85.8 all-gather.12
  226.7 85.8 all-gather.6
  314.9 85.8 all-gather.8
  648.5 144.5 reduce-scatter.4
  796.7 112.2 reduce-scatter.2
